TPU v7x, 128 devices: a whole 4x4x4 slice. The times are simulated.
128 devices in a mesh: expert: 4 (over y), shard: 32 (over z, x, core).
Axes of the slice: x: 4, y: 4, z: 4, core: 2. Of those that a mesh axis runs over, the one named last changes fastest.
Arguments:
- master_gate: float32 [64, 2048, 1408], P('expert', 'shard'), may hold values from -0.25 to 0.25
- master_up: float32 [64, 2048, 1408], P('expert', 'shard'), may hold values from -0.25 to 0.25
- master_down: float32 [64, 1408, 2048], P('expert', None, 'shard'), may hold values from -0.3125 to 0.3125
- router_weight: float32 [2048, 64], P('shard', 'expert'), may hold values from -0.125 to 0.125
- router_gain: float32 [2048], P('shard'), may hold values from 0.25 to 1.75
Outputs:
- final_gate: bfloat16 [64, 2048, 1408], P('expert', None, 'shard')
- final_up: bfloat16 [64, 2048, 1408], P('expert', None, 'shard')
- final_down: bfloat16 [64, 1408, 2048], P('expert', 'shard')
- scale_gate: float32 [64, 1408], P('expert', 'shard')
- scale_up: float32 [64, 1408], P('expert', 'shard')
- scale_down: float32 [64, 1408], P('expert', 'shard')
- serve_router: bfloat16 [2048, 64], replicated
All inputs are finite; a program needn't handle non-finite values. Where the computation divides by a largest or mean magnitude, that divisor is 1e-20 or more.
Results may differ from a plain program's by a relative error of at most 0.001.
Values may be sent and summed in bfloat16 or wider, within the bound.
A program may use at most 192 MiB of HBM per device.

v0:
```python
import jax
import jax.numpy as jnp
from jax import lax
from jax.experimental import pallas as pl
from jax.experimental.pallas import tpu as pltpu
from jax.sharding import PartitionSpec as P

MESH = pl.DeviceIdType.MESH
E, R, C, K = 16, 64, 1408, 44
S = 32
LT = C // 128
NT = 2 * LT
OUT = pltpu.VMEM
PIECE = K * 8
CHIPS = [(1, 0), (0, 1), (3, 0), (0, 3), (2, 2), (1, 1), (3, 3), (1, 3), (3, 1), (2, 1), (1, 2), (2, 3), (3, 2), (2, 0), (0, 2)]
OFFSETS = [(z, x, 0) for z, x in CHIPS] + [(z, x, 1) for z, x in CHIPS] + [(0, 0, 1)]


def target(me, offset):
    z, x, core = me // 8, (me // 2) % 4, me % 2
    return ((z + offset[0]) % 4) * 8 + ((x + offset[1]) % 4) * 2 + (core + offset[2]) % 2


def await_bytes(ref, sem):
    pltpu.make_async_copy(ref, ref, sem).wait()


def send_to(src, dst, send, recv, ex, to):
    pltpu.make_async_remote_copy(
        src_ref=src, dst_ref=dst, send_sem=send, recv_sem=recv, device_id=(ex, to), device_id_type=MESH
    ).start()


def relay_kernel(
    gate, up, down, weight, gain, pieces, routers, scale,
    x, turned, block, tops, landed, part, router,
    load, in_send, in_recv, out_send, out_recv, send, recv, r_send, r_recv, y_send, y_recv,
):
    me, ex = lax.axis_index("shard"), lax.axis_index("expert")
    loads = [pltpu.make_async_copy(src, x.at[a], load.at[a]) for a, src in enumerate((gate, up, down))]
    for copy in loads:
        copy.start()
    barrier = pltpu.get_barrier_semaphore()
    for offset in OFFSETS:
        pl.semaphore_signal(barrier, inc=1, device_id=(ex, target(me, offset)), device_id_type=MESH)
    for i in range(1, 4):
        pl.semaphore_signal(barrier, inc=1, device_id=((ex + i) % 4, me), device_id_type=MESH)
    scaled = weight[...] * gain[...]
    part[...] = jnp.concatenate([scaled, jnp.zeros_like(scaled)], axis=1).astype(jnp.bfloat16)
    router[me] = part[...]

    for a in range(3):
        loads[a].wait()

        def largest(i, _):
            lanes = pl.ds(pl.multiple_of(i * 128, 128), 128)
            for half in range(2):
                tops[a, half * LT + i] = jnp.max(jnp.abs(x[a, 8 * half : 8 * half + 8, :, lanes]), axis=1)
            return 0

        lax.fori_loop(0, LT, largest, 0)
        if a == 0:
            pl.semaphore_wait(barrier, S + 2)

        def give(i, _):
            to = (me + i) % S

            @pl.when(to < NT)
            def _():
                send_to(tops.at[a, to], landed.at[a, me], in_send, in_recv.at[a], ex, to)

            return 0

        lax.fori_loop(1, S, give, 0)

    def reduced(a, _):
        @pl.when(me < NT)
        def _():
            landed[a, me] = tops[a, me]
            await_bytes(landed.at[a, pl.ds(0, S - 1)], in_recv.at[a])
            scale[a, me] = jnp.max(landed[a], axis=0)

            def tell(i, _):
                send_to(scale.at[a, me], scale.at[a, me], out_send, out_recv.at[a], ex, (me + i) % S)
                return 0

            lax.fori_loop(1, S, tell, 0)

        return 0

    lax.fori_loop(0, 3, reduced, 0)

    def share(i, _):
        send_to(part, router.at[me], r_send, r_recv, ex, (me + i) % S)
        return 0

    lax.fori_loop(1, S, share, 0)

    def serve(a, _):
        @pl.when(me < NT)
        def _():
            await_bytes(scale.at[a, pl.ds(0, NT - 1)], out_recv.at[a])

        @pl.when(me >= NT)
        def _():
            await_bytes(scale.at[a], out_recv.at[a])

        def turn(i, _):
            lanes = pl.ds(pl.multiple_of(i * 128, 128), 128)
            by = [1.0 / scale[a, half * LT + i] for half in range(2)]
            for p in range(8):
                rows = [x[a, p + 8 * half, :, lanes] * by[half][p : p + 1] for half in range(2)]
                block[pl.ds(p, 128, stride=8)] = jnp.concatenate(rows, axis=0).T
            turned[a, pl.ds(pl.multiple_of(i * 1024, 1024), 1024)] = block[...].astype(jnp.bfloat16)
            return 0

        lax.fori_loop(0, LT, turn, 0)
        for offset in OFFSETS:
            to = target(me, offset)
            rows = pl.ds(pl.multiple_of(to * PIECE, PIECE), PIECE)
            send_to(turned.at[a, rows], pieces.at[a, me], send, recv, ex, to)
        pieces[a, me] = turned[a, pl.ds(pl.multiple_of(me * PIECE, PIECE), PIECE)]
        return 0

    lax.fori_loop(0, 3, serve, 0)
    await_bytes(router.at[pl.ds(0, S - 1)], r_recv)
    for i in range(1, 4):
        pltpu.make_async_remote_copy(
            src_ref=router, dst_ref=routers.at[ex], send_sem=y_send, recv_sem=y_recv,
            device_id=((ex + i) % 4, me), device_id_type=MESH,
        ).start()
    routers[ex] = router[...]

    @pl.when(me < NT)
    def _():
        await_bytes(tops.at[:, pl.ds(0, NT - 1)], in_send)
        await_bytes(landed.at[:, pl.ds(0, S - 1)], out_send)

    @pl.when(me >= NT)
    def _():
        await_bytes(tops, in_send)

    await_bytes(router.at[pl.ds(0, S - 1)], r_send)
    await_bytes(routers.at[pl.ds(0, 3)], y_send)
    await_bytes(routers.at[pl.ds(0, 3)], y_recv)
    await_bytes(pieces.at[:, pl.ds(0, S - 1)], send)
    await_bytes(pieces.at[:, pl.ds(0, S - 1)], recv)


def relay(gate, up, down, weight, gain):
    hbm, vmem = pl.BlockSpec(memory_space=pltpu.HBM), pl.BlockSpec(memory_space=pltpu.VMEM)
    dma = pltpu.SemaphoreType.DMA
    return pl.pallas_call(
        relay_kernel,
        name="relay",
        in_specs=[hbm, hbm, hbm, vmem, vmem],
        out_specs=[vmem, vmem, vmem],
        out_shape=[
            OUT((3, S, PIECE, 128), jnp.bfloat16),
            OUT((4, S, E, 128), jnp.bfloat16),
            OUT((3, NT, 8, 128), jnp.float32),
        ],
        scratch_shapes=[
            pltpu.VMEM((3, E, R, C), jnp.float32),
            pltpu.VMEM((3, C * 8, 128), jnp.bfloat16),
            pltpu.VMEM((1024, 128), jnp.float32),
            pltpu.VMEM((3, NT, 8, 128), jnp.float32),
            pltpu.VMEM((3, S, 8, 128), jnp.float32),
            pltpu.VMEM((E, 128), jnp.bfloat16),
            pltpu.VMEM((S, E, 128), jnp.bfloat16),
            dma((3,)), dma, dma((3,)), dma, dma((3,)), dma, dma, dma, dma, dma, dma,
        ],
        compiler_params=pltpu.CompilerParams(
            collective_id=0, has_side_effects=True, vmem_limit_bytes=40 * 2**20
        ),
    )(gate, up, down, weight, gain)


def halves(a, b):
    left = lax.broadcasted_iota(jnp.int32, a.shape, a.ndim - 1) < 64
    return jnp.where(left, a, pltpu.roll(b, 64, a.ndim - 1)), jnp.where(left, pltpu.roll(a, 64, a.ndim - 1), b)


def merge_kernel(width, pieces, routers, scale, gate, up, down, s_gate, s_up, s_down, serve):
    step = pl.program_id(0) * width
    for a, out in enumerate((gate, up, down)):
        for j in range(width):
            pair = [pieces[a, 2 * (step + j) + i].astype(jnp.float32) for i in range(2)]
            low, high = halves(*pair)
            both = jnp.concatenate([low.reshape(K, 8, 128), high.reshape(K, 8, 128)], axis=1)
            out[:, :, 128 * j : 128 * j + 128] = both.astype(jnp.bfloat16)
    for j in range(width):
        pair = [routers[:, 2 * (step + j) + i].astype(jnp.float32).reshape(64, 128) for i in range(2)]
        serve[:, 128 * j : 128 * j + 128] = halves(*pair)[0].astype(jnp.bfloat16)

    @pl.when(pl.program_id(0) == 0)
    def _():
        start = lax.axis_index("shard") * K
        for a, out in enumerate((s_gate, s_up, s_down)):
            rows = [jnp.concatenate([scale[a, half * LT + i] for i in range(LT)], axis=1) for half in range(2)]
            out[...] = pltpu.roll(jnp.concatenate(rows, axis=0), (C - start) % C, 1)[:, :K]


def merge(pieces, routers, scale):
    width = 2
    wide = pl.BlockSpec((K, E, 128 * width), lambda i: (0, 0, i))
    small = pl.BlockSpec((E, K), lambda i: (0, 0))
    vmem = pl.BlockSpec(memory_space=pltpu.VMEM)
    return pl.pallas_call(
        lambda *refs: merge_kernel(width, *refs),
        name="merge",
        grid=(16 // width,),
        in_specs=[vmem, vmem, vmem],
        out_specs=[wide] * 3 + [small] * 3 + [pl.BlockSpec((64, 128 * width), lambda i: (0, i))],
        out_shape=[jax.ShapeDtypeStruct((K, E, 2048), jnp.bfloat16)] * 3
        + [jax.ShapeDtypeStruct((E, K), jnp.float32)] * 3
        + [jax.ShapeDtypeStruct((64, 2048), jnp.bfloat16)],
        compiler_params=pltpu.CompilerParams(vmem_limit_bytes=16 * 2**20),
    )(pieces, routers, scale)


def body(master_gate, master_up, master_down, router_weight, router_gain):
    masters = (master_gate, master_up, jnp.swapaxes(master_down, 1, 2))
    pieces, routers, scale = relay(*masters, router_weight.T, router_gain[None])
    gate, up, down, s_gate, s_up, s_down, serve = merge(pieces, routers, scale)
    return (
        jnp.transpose(gate, (1, 2, 0)),
        jnp.transpose(up, (1, 2, 0)),
        jnp.transpose(down, (1, 0, 2)),
        s_gate,
        s_up,
        s_down,
        serve.T,
    )


def solution(mesh):
    return jax.shard_map(
        body,
        mesh=mesh,
        in_specs=(
            P("expert", "shard", None),
            P("expert", "shard", None),
            P("expert", None, "shard"),
            P("shard", "expert"),
            P("shard"),
        ),
        out_specs=(
            P("expert", None, "shard"),
            P("expert", None, "shard"),
            P("expert", "shard", None),
            P("expert", "shard"),
            P("expert", "shard"),
            P("expert", "shard"),
            P(),
        ),
        check_vma=False,
    )
```

profile of v0, /device:TPU:1, one launch (start us, length us, event | category | flops | bytes accessed | tf_op | source)
XLA Modules:
  0.0 135.0 jit_solution(5125918986462891227)
XLA Ops:
  0.6 0.0 copy-start
  0.6 0.7 copy-done
  1.3 0.0 copy-start.1
  1.3 0.7 copy-done.1
  2.0 126.6 %relay.1 = (bf16[3,32,352,128]{3,2,1,0:T(8,128)(2,1)S(1)}, bf16[4,32,16,128]{3,2,1,0:T(8,128)(2,1)S(1)}, f32[3,22,8,128]{3,2,1,0:T(8,128)S(1)}) custom-call(f32[16,64,1408]{2,1,0:T(8,128)} %gate.1, f32[16,64,1408]{2,1,0:T(8,128)} %up.1, f32[16,64,1408]{2,1,0:T(8,128)} %bitcast.9, f32[16,64]{1,0:T(8,128)S(1)} %bitcast.7, f32[1,64]{1,0:T(1,128)S(1)} %bitcast.8), custom_call_target="tpu_custom_call" | custom-call | tf_op jit(solution)/shard_map/relay/pallas_call | solution.py:153
  128.6 6.4 %merge.1 = (bf16[44,16,2048]{2,1,0:T(8,128)(2,1)}, bf16[44,16,2048]{2,1,0:T(8,128)(2,1)}, bf16[44,16,2048]{2,1,0:T(8,128)(2,1)}, f32[16,44]{1,0:T(8,128)}, f32[1...) custom-call(bf16[3,32,352,128]{3,2,1,0:T(8,128)(2,1)S(1)} %get-tuple-element.17.refs_0_, ...), custom_call_target="tpu_custom_call" | custom-call | tf_op jit(solution)/shard_map/merge/pallas_call | solution.py:209
Async XLA Ops:
  0.6 0.7 copy-start
  1.3 0.7 copy-start.1
where the time goes:
time: 135 us
  Pallas kernels  133 us (99%)
    pallas_call x1, Pallas kernels, relay(): pl.pallas_call(relay_kernel, name='relay', in_specs=[hbm, hbm, hbm, vmem,...  127 us
    pallas_call x1, Pallas kernels, merge(): pl.pallas_call(lambda *refs: merge_kernel(width, *refs), name='merge', gr...  6.37 us

commit v1 on v0

v1 whole, which is shorter than its diff:
```python
import jax
import jax.numpy as jnp
from jax import lax
from jax.experimental import pallas as pl
from jax.experimental.pallas import tpu as pltpu
from jax.sharding import PartitionSpec as P

MESH = pl.DeviceIdType.MESH
E, R, C, K = 16, 64, 1408, 44
S = 32
LT = C // 128
NT = 2 * LT
OUT = pltpu.VMEM
PIECE = K * 8
CHIPS = [(1, 1), (3, 3), (0, 1), (1, 3), (3, 1), (0, 3), (1, 0), (3, 0), (2, 0), (1, 2), (3, 2), (2, 2), (2, 1), (0, 2), (2, 3)]
OFFSETS = [(z, x, 0) for z, x in CHIPS] + [(z, x, 1) for z, x in CHIPS] + [(0, 0, 1)]


def target(me, offset):
    z, x, core = me // 8, (me // 2) % 4, me % 2
    return ((z + offset[0]) % 4) * 8 + ((x + offset[1]) % 4) * 2 + (core + offset[2]) % 2


def await_bytes(ref, sem):
    pltpu.make_async_copy(ref, ref, sem).wait()


def send_to(src, dst, send, recv, ex, to):
    pltpu.make_async_remote_copy(
        src_ref=src, dst_ref=dst, send_sem=send, recv_sem=recv, device_id=(ex, to), device_id_type=MESH
    ).start()


def halves(a, b):
    left = lax.broadcasted_iota(jnp.int32, a.shape, a.ndim - 1) < 64
    return jnp.where(left, a, pltpu.roll(b, 64, a.ndim - 1)), jnp.where(left, pltpu.roll(a, 64, a.ndim - 1), b)


def side_by_side(a, b):
    low, high = halves(a.astype(jnp.float32), b.astype(jnp.float32))
    both = jnp.concatenate([low.reshape(K, 8, 128), high.reshape(K, 8, 128)], axis=1)
    return both.astype(jnp.bfloat16)


def relay_kernel(
    gate, up, down, weight_in, gain_in, pieces, merged, routers, scale,
    x, weight, gain, turned, block, tops, landed, part, router,
    load, in_send, in_recv, out_send, out_recv, send, recv, r_send, r_recv, y_send, y_recv,
):
    me, ex = lax.axis_index("shard"), lax.axis_index("expert")
    firsts = [pltpu.make_async_copy(gate.at[pl.ds(8 * h, 8)], x.at[0, pl.ds(8 * h, 8)], load.at[h]) for h in range(2)]
    lates = [pltpu.make_async_copy(src, x.at[a], load.at[a + 1]) for a, src in ((1, up), (2, down))]
    smalls = [
        pltpu.make_async_copy(weight_in, weight, load.at[4]),
        pltpu.make_async_copy(gain_in, gain, load.at[5]),
    ]
    for copy in firsts + smalls:
        copy.start()
    barrier = pltpu.get_barrier_semaphore()
    for offset in OFFSETS:
        pl.semaphore_signal(barrier, inc=1, device_id=(ex, target(me, offset)), device_id_type=MESH)
    for i in range(1, 4):
        pl.semaphore_signal(barrier, inc=1, device_id=((ex + i) % 4, me), device_id_type=MESH)
    def largest(a, half):
        def one(i, _):
            lanes = pl.ds(pl.multiple_of(i * 128, 128), 128)
            tops[a, half * LT + i] = jnp.max(jnp.abs(x[a, 8 * half : 8 * half + 8, :, lanes]), axis=1)
            return 0

        lax.fori_loop(0, LT, one, 0)

    def give(a, half):
        def one(i, _):
            to = half * LT + (me + i) % LT

            @pl.when(to != me)
            def _():
                send_to(tops.at[a, to], landed.at[a, me], in_send, in_recv.at[a], ex, to)

            return 0

        lax.fori_loop(0, LT, one, 0)

    for half in range(2):
        firsts[half].wait()
        lates[half].start()
        largest(0, half)
        if half == 0:
            pl.semaphore_wait(barrier, S + 2)
        give(0, half)
    for a in (1, 2):
        lates[a - 1].wait()
        for half in range(2):
            largest(a, half)
            give(a, half)

    def reduced(a, _):
        @pl.when(me < NT)
        def _():
            landed[a, me] = tops[a, me]
            await_bytes(landed.at[a, pl.ds(0, S - 1)], in_recv.at[a])
            scale[a, me] = jnp.max(landed[a], axis=0)

            def tell(i, _):
                send_to(scale.at[a, me], scale.at[a, me], out_send, out_recv.at[a], ex, (me + i) % S)
                return 0

            lax.fori_loop(1, S, tell, 0)

        return 0

    lax.fori_loop(0, 3, reduced, 0)

    for copy in smalls:
        copy.wait()
    scaled = weight[...] * gain[...]
    part[...] = jnp.concatenate([scaled, jnp.zeros_like(scaled)], axis=1).astype(jnp.bfloat16)
    router[me] = part[...]

    def share(i, _):
        send_to(part, router.at[me], r_send, r_recv, ex, (me + i) % S)
        return 0

    lax.fori_loop(1, S, share, 0)

    def serve(a, _):
        @pl.when(me < NT)
        def _():
            await_bytes(scale.at[a, pl.ds(0, NT - 1)], out_recv.at[a])

        @pl.when(me >= NT)
        def _():
            await_bytes(scale.at[a], out_recv.at[a])

        def turn(i, _):
            lanes = pl.ds(pl.multiple_of(i * 128, 128), 128)
            by = [1.0 / scale[a, half * LT + i] for half in range(2)]
            for p in range(8):
                rows = [x[a, p + 8 * half, :, lanes] * by[half][p : p + 1] for half in range(2)]
                block[pl.ds(p, 128, stride=8)] = jnp.concatenate(rows, axis=0).T
            turned[a, pl.ds(pl.multiple_of(i * 1024, 1024), 1024)] = block[...].astype(jnp.bfloat16)
            return 0

        lax.fori_loop(0, LT, turn, 0)
        for offset in OFFSETS:
            to = target(me, offset)
            rows = pl.ds(pl.multiple_of(to * PIECE, PIECE), PIECE)
            send_to(turned.at[a, rows], pieces.at[a, me], send, recv.at[a], ex, to)
        pieces[a, me] = turned[a, pl.ds(pl.multiple_of(me * PIECE, PIECE), PIECE)]
        return 0

    lax.fori_loop(0, 3, serve, 0)
    await_bytes(router.at[pl.ds(0, S - 1)], r_recv)
    for i in range(1, 4):
        pltpu.make_async_remote_copy(
            src_ref=router, dst_ref=routers.at[ex], send_sem=y_send, recv_sem=y_recv,
            device_id=((ex + i) % 4, me), device_id_type=MESH,
        ).start()
    routers[ex] = router[...]

    def join(a, _):
        await_bytes(pieces.at[a, pl.ds(0, S - 1)], recv.at[a])

        def pair(j, _):
            lanes = pl.ds(pl.multiple_of(j * 128, 128), 128)
            merged[a, :, :, lanes] = side_by_side(pieces[a, 2 * j], pieces[a, 2 * j + 1])
            return 0

        lax.fori_loop(0, S // 2, pair, 0)
        return 0

    lax.fori_loop(0, 2, join, 0)

    @pl.when(me < NT)
    def _():
        await_bytes(tops.at[:, pl.ds(0, NT - 1)], in_send)
        await_bytes(landed.at[:, pl.ds(0, S - 1)], out_send)

    @pl.when(me >= NT)
    def _():
        await_bytes(tops, in_send)

    await_bytes(router.at[pl.ds(0, S - 1)], r_send)
    await_bytes(routers.at[pl.ds(0, 3)], y_send)
    await_bytes(routers.at[pl.ds(0, 3)], y_recv)
    await_bytes(pieces.at[:, pl.ds(0, S - 1)], send)
    await_bytes(pieces.at[2, pl.ds(0, S - 1)], recv.at[2])


def relay(gate, up, down, weight, gain):
    hbm, vmem = pl.BlockSpec(memory_space=pltpu.HBM), pl.BlockSpec(memory_space=pltpu.VMEM)
    dma = pltpu.SemaphoreType.DMA
    return pl.pallas_call(
        relay_kernel,
        name="relay",
        in_specs=[hbm] * 5,
        out_specs=[vmem] * 4,
        out_shape=[
            OUT((3, S, PIECE, 128), jnp.bfloat16),
            OUT((2, K, E, 2048), jnp.bfloat16),
            OUT((4, S, E, 128), jnp.bfloat16),
            OUT((3, NT, 8, 128), jnp.float32),
        ],
        scratch_shapes=[
            pltpu.VMEM((3, E, R, C), jnp.float32),
            pltpu.VMEM((E, R), jnp.float32),
            pltpu.VMEM((1, R), jnp.float32),
            pltpu.VMEM((3, C * 8, 128), jnp.bfloat16),
            pltpu.VMEM((1024, 128), jnp.float32),
            pltpu.VMEM((3, NT, 8, 128), jnp.float32),
            pltpu.VMEM((3, S, 8, 128), jnp.float32),
            pltpu.VMEM((E, 128), jnp.bfloat16),
            pltpu.VMEM((S, E, 128), jnp.bfloat16),
            dma((6,)), dma, dma((3,)), dma, dma((3,)), dma, dma((3,)), dma, dma, dma, dma,
        ],
        compiler_params=pltpu.CompilerParams(
            collective_id=0, has_side_effects=True, vmem_limit_bytes=40 * 2**20
        ),
    )(gate, up, down, weight, gain)


def finish_kernel(pieces, merged, routers, scale, gate, up, down, s_gate, s_up, s_down, serve, last, out_sem):
    outs = [pltpu.make_async_copy(merged.at[a], out, out_sem.at[a]) for a, out in enumerate((gate, up))]
    for copy in outs:
        copy.start()

    for part in range(4):

        def pair(j, _):
            lanes = pl.ds(pl.multiple_of(j * 128, 128), 128)
            last[:, :, lanes] = side_by_side(pieces[2, 2 * j], pieces[2, 2 * j + 1])
            return 0

        lax.fori_loop(4 * part, 4 * part + 4, pair, 0)
        lanes = pl.ds(512 * part, 512)
        outs.append(pltpu.make_async_copy(last.at[:, :, lanes], down.at[:, :, lanes], out_sem.at[2 + part]))
        outs[-1].start()
    for j in range(S // 2):
        both = [routers[:, 2 * j + i].astype(jnp.float32).reshape(64, 128) for i in range(2)]
        serve[:, 128 * j : 128 * j + 128] = halves(*both)[0].astype(jnp.bfloat16)
    start = lax.axis_index("shard") * K
    for a, out in enumerate((s_gate, s_up, s_down)):
        rows = [jnp.concatenate([scale[a, half * LT + i] for i in range(LT)], axis=1) for half in range(2)]
        out[...] = pltpu.roll(jnp.concatenate(rows, axis=0), (C - start) % C, 1)[:, :K]
    for copy in outs:
        copy.wait()


def finish(pieces, merged, routers, scale):
    hbm, vmem = pl.BlockSpec(memory_space=pltpu.HBM), pl.BlockSpec(memory_space=pltpu.VMEM)
    return pl.pallas_call(
        finish_kernel,
        name="finish",
        in_specs=[vmem] * 4,
        out_specs=[hbm] * 3 + [vmem] * 4,
        out_shape=[jax.ShapeDtypeStruct((K, E, 2048), jnp.bfloat16)] * 3
        + [jax.ShapeDtypeStruct((E, K), jnp.float32)] * 3
        + [jax.ShapeDtypeStruct((64, 2048), jnp.bfloat16)],
        scratch_shapes=[pltpu.VMEM((K, E, 2048), jnp.bfloat16), pltpu.SemaphoreType.DMA((6,))],
        compiler_params=pltpu.CompilerParams(vmem_limit_bytes=12 * 2**20),
    )(pieces, merged, routers, scale)


def body(master_gate, master_up, master_down, router_weight, router_gain):
    masters = (master_gate, master_up, jnp.swapaxes(master_down, 1, 2))
    pieces, merged, routers, scale = relay(*masters, router_weight.T, router_gain[None])
    gate, up, down, s_gate, s_up, s_down, serve = finish(pieces, merged, routers, scale)
    return (
        jnp.transpose(gate, (1, 2, 0)),
        jnp.transpose(up, (1, 2, 0)),
        jnp.transpose(down, (1, 0, 2)),
        s_gate,
        s_up,
        s_down,
        serve.T,
    )


def solution(mesh):
    return jax.shard_map(
        body,
        mesh=mesh,
        in_specs=(
            P("expert", "shard", None),
            P("expert", "shard", None),
            P("expert", None, "shard"),
            P("shard", "expert"),
            P("shard"),
        ),
        out_specs=(
            P("expert", None, "shard"),
            P("expert", None, "shard"),
            P("expert", "shard", None),
            P("expert", "shard"),
            P("expert", "shard"),
            P("expert", "shard"),
            P(),
        ),
        check_vma=False,
    )
```

time: 135 us -> 123 us (0.911)
  Pallas kernels: 133 us -> 122 us
    pallas_call x2, Pallas kernels: 133 us -> 122 us  [the longest x1 118 us: relay(): pl.pallas_call(relay_kernel, name='relay', in_specs=[hbm] * 5, out_specs=...]
where the time goes in v1:
time: 123 us
  Pallas kernels  122 us (99%)
    pallas_call x1, Pallas kernels, relay(): pl.pallas_call(relay_kernel, name='relay', in_specs=[hbm] * 5, out_specs=...  118 us
    pallas_call x1, Pallas kernels, finish(): pl.pallas_call(finish_kernel, name='finish', in_specs=[vmem] * 4, out_spe...  4.17 us

profile of v1, /device:TPU:1, one launch (start us, length us, event | category | flops | bytes accessed | tf_op | source)
XLA Modules:
  0.0 122.9 jit_solution(6523385341501600018)
XLA Ops:
  0.6 118.1 %relay.1 = (bf16[3,32,352,128]{3,2,1,0:T(8,128)(2,1)S(1)}, bf16[2,44,16,2048]{3,2,1,0:T(8,128)(2,1)S(1)}, bf16[4,32,16,128]{3,2,1,0:T(8,128)(2,1)S(1)}, f32[3,22,8,128]{3,2,1,0:T(8,128)S(1)}) custom-call(f32[16,64,1408]{2,1,0:T(8,128)} %gate.1, f32[16,64,1408]{2,1,0:T(8,128)} %up.1, f32[16,64,1408]{2,1,0:T(8,128)} %bitcast.7, f32[16,64]{1,0:T(8,128)} %bitcast.8, ...), custom_call_target="tpu_custom_call" | custom-call | tf_op jit(solution)/shard_map/relay/pallas_call | solution.py:193
  118.7 4.2 %finish.1 = (bf16[44,16,2048]{2,1,0:T(8,128)(2,1)}, bf16[44,16,2048]{2,1,0:T(8,128)(2,1)}, bf16[44,16,2048]{2,1,0:T(8,128)(2,1)}, f32[16,44]{1,0:T(8,128)}, f32[...) custom-call(bf16[3,32,352,128]{3,2,1,0:T(8,128)(2,1)S(1)} %get-tuple-element.18.pieces, ...), custom_call_target="tpu_custom_call" | custom-call | tf_op jit(solution)/shard_map/finish/pallas_call | solution.py:251

commit v2 on v1

--- a/solution.py
+++ b/solution.py
@@ -12,7 +12,7 @@
 NT = 2 * LT
 OUT = pltpu.VMEM
 PIECE = K * 8
-CHIPS = [(1, 1), (3, 3), (0, 1), (1, 3), (3, 1), (0, 3), (1, 0), (3, 0), (2, 0), (1, 2), (3, 2), (2, 2), (2, 1), (0, 2), (2, 3)]
+CHIPS = [(1, 1), (3, 3), (0, 1), (1, 3), (3, 1), (0, 3), (2, 0), (1, 0), (3, 0), (2, 2), (1, 2), (3, 2), (2, 1), (0, 2), (2, 3)]
 OFFSETS = [(z, x, 0) for z, x in CHIPS] + [(z, x, 1) for z, x in CHIPS] + [(0, 0, 1)]
 
 
@@ -132,16 +132,16 @@
         def _():
             await_bytes(scale.at[a], out_recv.at[a])
 
-        def turn(i, _):
-            lanes = pl.ds(pl.multiple_of(i * 128, 128), 128)
+        def turn(i, block):
+            lanes = pl.ds(i * 128, 128)
             by = [1.0 / scale[a, half * LT + i] for half in range(2)]
             for p in range(8):
                 rows = [x[a, p + 8 * half, :, lanes] * by[half][p : p + 1] for half in range(2)]
                 block[pl.ds(p, 128, stride=8)] = jnp.concatenate(rows, axis=0).T
-            turned[a, pl.ds(pl.multiple_of(i * 1024, 1024), 1024)] = block[...].astype(jnp.bfloat16)
-            return 0
-
-        lax.fori_loop(0, LT, turn, 0)
+            turned[a, pl.ds(i * 1024, 1024)] = block[...].astype(jnp.bfloat16)
+
+        for i in range(LT):
+            turn(i, block.at[i % 2])
         for offset in OFFSETS:
             to = target(me, offset)
             rows = pl.ds(pl.multiple_of(to * PIECE, PIECE), PIECE)
@@ -206,7 +206,7 @@
             pltpu.VMEM((E, R), jnp.float32),
             pltpu.VMEM((1, R), jnp.float32),
             pltpu.VMEM((3, C * 8, 128), jnp.bfloat16),
-            pltpu.VMEM((1024, 128), jnp.float32),
+            pltpu.VMEM((2, 1024, 128), jnp.float32),
             pltpu.VMEM((3, NT, 8, 128), jnp.float32),
             pltpu.VMEM((3, S, 8, 128), jnp.float32),
             pltpu.VMEM((E, 128), jnp.bfloat16),

time: 123 us -> 122 us (level)
  no operation moved by 1% of the time
where the time goes in v2:
time: 122 us
  Pallas kernels  121 us (99%)
    pallas_call x1, Pallas kernels, relay(): pl.pallas_call(relay_kernel, name='relay', in_specs=[hbm] * 5, out_specs=...  117 us
    pallas_call x1, Pallas kernels, finish(): pl.pallas_call(finish_kernel, name='finish', in_specs=[vmem] * 4, out_spe...  4.17 us

profile of v2, /device:TPU:1, one launch (start us, length us, event | category | flops | bytes accessed | tf_op | source)
XLA Modules:
  0.0 121.8 jit_solution(15577979598609125194)
XLA Ops:
  0.6 117.0 %relay.1 = (bf16[3,32,352,128]{3,2,1,0:T(8,128)(2,1)S(1)}, bf16[2,44,16,2048]{3,2,1,0:T(8,128)(2,1)S(1)}, bf16[4,32,16,128]{3,2,1,0:T(8,128)(2,1)S(1)}, f32[3,22,8,128]{3,2,1,0:T(8,128)S(1)}) custom-call(f32[16,64,1408]{2,1,0:T(8,128)} %gate.1, f32[16,64,1408]{2,1,0:T(8,128)} %up.1, f32[16,64,1408]{2,1,0:T(8,128)} %bitcast.7, f32[16,64]{1,0:T(8,128)} %bitcast.8, ...), custom_call_target="tpu_custom_call" | custom-call | tf_op jit(solution)/shard_map/relay/pallas_call | solution.py:193
  117.6 4.2 %finish.1 = (bf16[44,16,2048]{2,1,0:T(8,128)(2,1)}, bf16[44,16,2048]{2,1,0:T(8,128)(2,1)}, bf16[44,16,2048]{2,1,0:T(8,128)(2,1)}, f32[16,44]{1,0:T(8,128)}, f32[...) custom-call(bf16[3,32,352,128]{3,2,1,0:T(8,128)(2,1)S(1)} %get-tuple-element.18.pieces, ...), custom_call_target="tpu_custom_call" | custom-call | tf_op jit(solution)/shard_map/finish/pallas_call | solution.py:251

commit v3 on v2

--- a/solution.py
+++ b/solution.py
@@ -38,13 +38,13 @@
 
 def side_by_side(a, b):
     low, high = halves(a.astype(jnp.float32), b.astype(jnp.float32))
-    both = jnp.concatenate([low.reshape(K, 8, 128), high.reshape(K, 8, 128)], axis=1)
+    both = jnp.concatenate([v.reshape(-1, 8, 128) for v in (low, high)], axis=1)
     return both.astype(jnp.bfloat16)
 
 
 def relay_kernel(
-    gate, up, down, weight_in, gain_in, pieces, merged, routers, scale,
-    x, weight, gain, turned, block, tops, landed, part, router,
+    gate, up, down, weight_in, gain_in, pieces, merged, whole, mine,
+    routers, scale, x, weight, gain, turned, block, tops, landed, part, router,
     load, in_send, in_recv, out_send, out_recv, send, recv, r_send, r_recv, y_send, y_recv,
 ):
     me, ex = lax.axis_index("shard"), lax.axis_index("expert")
@@ -170,6 +170,14 @@
         return 0
 
     lax.fori_loop(0, 2, join, 0)
+    await_bytes(routers.at[pl.ds(0, 3)], y_recv)
+    for j in range(S // 2):
+        both = [routers[:, 2 * j + i].astype(jnp.float32).reshape(64, 128) for i in range(2)]
+        whole[:, 128 * j : 128 * j + 128] = halves(*both)[0].astype(jnp.bfloat16)
+    start = me * K
+    for a in range(3):
+        rows = [jnp.concatenate([scale[a, half * LT + i] for i in range(LT)], axis=1) for half in range(2)]
+        mine[a] = pltpu.roll(jnp.concatenate(rows, axis=0), (C - start) % C, 1)[:, :128]
 
     @pl.when(me < NT)
     def _():
@@ -182,7 +190,6 @@
 
     await_bytes(router.at[pl.ds(0, S - 1)], r_send)
     await_bytes(routers.at[pl.ds(0, 3)], y_send)
-    await_bytes(routers.at[pl.ds(0, 3)], y_recv)
     await_bytes(pieces.at[:, pl.ds(0, S - 1)], send)
     await_bytes(pieces.at[2, pl.ds(0, S - 1)], recv.at[2])
 
@@ -198,10 +205,12 @@
         out_shape=[
             OUT((3, S, PIECE, 128), jnp.bfloat16),
             OUT((2, K, E, 2048), jnp.bfloat16),
-            OUT((4, S, E, 128), jnp.bfloat16),
-            OUT((3, NT, 8, 128), jnp.float32),
+            OUT((64, 2048), jnp.bfloat16),
+            OUT((3, E, 128), jnp.float32),
         ],
         scratch_shapes=[
+            pltpu.VMEM((4, S, E, 128), jnp.bfloat16),
+            pltpu.VMEM((3, NT, 8, 128), jnp.float32),
             pltpu.VMEM((3, E, R, C), jnp.float32),
             pltpu.VMEM((E, R), jnp.float32),
             pltpu.VMEM((1, R), jnp.float32),
@@ -219,52 +228,48 @@
     )(gate, up, down, weight, gain)
 
 
-def finish_kernel(pieces, merged, routers, scale, gate, up, down, s_gate, s_up, s_down, serve, last, out_sem):
+def finish_kernel(pieces, merged, router, mine, gate, up, down, s_gate, s_up, s_down, serve, last, out_sem):
     outs = [pltpu.make_async_copy(merged.at[a], out, out_sem.at[a]) for a, out in enumerate((gate, up))]
+    outs.append(pltpu.make_async_copy(router, serve, out_sem.at[4]))
     for copy in outs:
         copy.start()
 
-    for part in range(4):
+    for part in range(2):
+        rows, columns = slice(part * PIECE // 2, (part + 1) * PIECE // 2), pl.ds(part * K // 2, K // 2)
 
         def pair(j, _):
             lanes = pl.ds(pl.multiple_of(j * 128, 128), 128)
-            last[:, :, lanes] = side_by_side(pieces[2, 2 * j], pieces[2, 2 * j + 1])
+            last[columns, :, lanes] = side_by_side(pieces[2, 2 * j, rows], pieces[2, 2 * j + 1, rows])
             return 0
 
-        lax.fori_loop(4 * part, 4 * part + 4, pair, 0)
-        lanes = pl.ds(512 * part, 512)
-        outs.append(pltpu.make_async_copy(last.at[:, :, lanes], down.at[:, :, lanes], out_sem.at[2 + part]))
+        lax.fori_loop(0, S // 2, pair, 0)
+        outs.append(pltpu.make_async_copy(last.at[columns], down.at[columns], out_sem.at[2 + part]))
         outs[-1].start()
-    for j in range(S // 2):
-        both = [routers[:, 2 * j + i].astype(jnp.float32).reshape(64, 128) for i in range(2)]
-        serve[:, 128 * j : 128 * j + 128] = halves(*both)[0].astype(jnp.bfloat16)
-    start = lax.axis_index("shard") * K
     for a, out in enumerate((s_gate, s_up, s_down)):
-        rows = [jnp.concatenate([scale[a, half * LT + i] for i in range(LT)], axis=1) for half in range(2)]
-        out[...] = pltpu.roll(jnp.concatenate(rows, axis=0), (C - start) % C, 1)[:, :K]
+        out[...] = mine[a, :, :K]
     for copy in outs:
         copy.wait()
 
 
-def finish(pieces, merged, routers, scale):
+def finish(pieces, merged, router, mine):
     hbm, vmem = pl.BlockSpec(memory_space=pltpu.HBM), pl.BlockSpec(memory_space=pltpu.VMEM)
     return pl.pallas_call(
         finish_kernel,
         name="finish",
         in_specs=[vmem] * 4,
-        out_specs=[hbm] * 3 + [vmem] * 4,
+        out_specs=[hbm] * 3 + [vmem] * 3 + [hbm],
         out_shape=[jax.ShapeDtypeStruct((K, E, 2048), jnp.bfloat16)] * 3
         + [jax.ShapeDtypeStruct((E, K), jnp.float32)] * 3
         + [jax.ShapeDtypeStruct((64, 2048), jnp.bfloat16)],
-        scratch_shapes=[pltpu.VMEM((K, E, 2048), jnp.bfloat16), pltpu.SemaphoreType.DMA((6,))],
+        scratch_shapes=[pltpu.VMEM((K, E, 2048), jnp.bfloat16), pltpu.SemaphoreType.DMA((5,))],
         compiler_params=pltpu.CompilerParams(vmem_limit_bytes=12 * 2**20),
-    )(pieces, merged, routers, scale)
+    )(pieces, merged, router, mine)
 
 
 def body(master_gate, master_up, master_down, router_weight, router_gain):
     masters = (master_gate, master_up, jnp.swapaxes(master_down, 1, 2))
-    pieces, merged, routers, scale = relay(*masters, router_weight.T, router_gain[None])
-    gate, up, down, s_gate, s_up, s_down, serve = finish(pieces, merged, routers, scale)
+    pieces, merged, router, mine = relay(*masters, router_weight.T, router_gain[None])
+    gate, up, down, s_gate, s_up, s_down, serve = finish(pieces, merged, router, mine)
     return (
         jnp.transpose(gate, (1, 2, 0)),
         jnp.transpose(up, (1, 2, 0)),

time: 122 us -> 123 us (level)
  no operation moved by 1% of the time
where the time goes in v3:
time: 123 us
  Pallas kernels  122 us (99%)
    pallas_call x1, Pallas kernels, relay(): pl.pallas_call(relay_kernel, name='relay', in_specs=[hbm] * 5, out_specs=...  117 us
    pallas_call x1, Pallas kernels, finish(): pl.pallas_call(finish_kernel, name='finish', in_specs=[vmem] * 4, out_spe...  4.89 us

profile of v3, /device:TPU:1, one launch (start us, length us, event | category | flops | bytes accessed | tf_op | source)
XLA Modules:
  0.0 122.6 jit_solution(8833399573093376259)
XLA Ops:
  0.6 117.1 %relay.1 = (bf16[3,32,352,128]{3,2,1,0:T(8,128)(2,1)S(1)}, bf16[2,44,16,2048]{3,2,1,0:T(8,128)(2,1)S(1)}, bf16[64,2048]{1,0:T(8,128)(2,1)S(1)}, f32[3,16,128]{2,1,0:T(8,128)S(1)}) custom-call(f32[16,64,1408]{2,1,0:T(8,128)} %gate.1, f32[16,64,1408]{2,1,0:T(8,128)} %up.1, f32[16,64,1408]{2,1,0:T(8,128)} %bitcast.7, f32[16,64]{1,0:T(8,128)} %bitcast.8, ...), custom_call_target="tpu_custom_call" | custom-call | tf_op jit(solution)/shard_map/relay/pallas_call | solution.py:200
  117.7 4.9 %finish.1 = (bf16[44,16,2048]{2,1,0:T(8,128)(2,1)}, bf16[44,16,2048]{2,1,0:T(8,128)(2,1)}, bf16[44,16,2048]{2,1,0:T(8,128)(2,1)}, f32[16,44]{1,0:T(8,128)}, f32[...) custom-call(bf16[3,32,352,128]{3,2,1,0:T(8,128)(2,1)S(1)} %get-tuple-element.18.pieces, ...), custom_call_target="tpu_custom_call" | custom-call | tf_op jit(solution)/shard_map/finish/pallas_call | solution.py:256
